TPU v7x, 512 devices: a whole 4x8x8 slice. The times are simulated.
512 devices in a mesh: range: 32 (over y_hi, z), depth: 16 (over x, y_lo, core).
Axes of the slice: x: 4, y: 8 (y_hi: 4, y_lo: 2; y = y_hi * 2 + y_lo), z: 8, core: 2. Of those that a mesh axis runs over, the one named last changes fastest.
Arguments:
- pressure: float32 [16384, 4096], P('depth', 'range'), may hold values from -6 to 6
- vel_range: float32 [16384, 4096], P('depth', 'range'), may hold values from -3 to 3
- vel_depth: float32 [16384, 4096], P('depth', 'range'), may hold values from -3 to 3
- sound_speed: float32 [16384, 4096], P('depth', 'range'), may hold values from 0.5 to 1.1
- density: float32 [16384, 4096], P('depth', 'range'), may hold values from 1 to 3
- ahead_speed: float32 [16384, 64], P('depth'), may hold values from 0.5 to 1.1
- ahead_density: float32 [16384, 64], P('depth'), may hold values from 1 to 3
- shifts: int32 [4], replicated, may hold values from 1 to 16, as said below
- sources: int32 [8, 2], replicated, may hold values from 0 to 16383, as said below
- wavelet: float32 [8, 4], replicated, may hold values from -12 to 12
Outputs:
- pressure_out: float32 [16384, 4096], P('depth', 'range')
- range_out: float32 [16384, 4096], P('depth', 'range')
- depth_out: float32 [16384, 4096], P('depth', 'range')
Inputs may be any that keep to these rules, and one draw needn't show every extreme that they name: `shifts`: every draw has a step that advances by exactly 16 columns. `sources`: column 0 is a depth index below 16384, column 1 a range index below 4096.
All inputs are finite; a program needn't handle non-finite values.
Results may differ from a plain program's by a relative error of at most 0.0003.
Values sent between devices are 32-bit elements; how exact they have to be, the bound alone decides.
A program may use at most 64 MiB of HBM per device.

v0:
```python
import jax
import jax.numpy as jnp
from jax import lax
from jax.sharding import PartitionSpec as P

ITERS = 4


TIME_STEP = 0.6


def shifted(shard, axis, by):
    size = lax.axis_size(axis)
    pairs = [(i, i + by) for i in range(size) if 0 <= i + by < size]
    return lax.ppermute(shard, axis, pairs)


def right_rims(pressure, density):
    return shifted((pressure[:, :1], density[:, :1]), "range", -1)


def lower_rims(pressure, density):
    return shifted((pressure[:1], density[:1]), "depth", -1)


def left_rims(column):
    return shifted(column, "range", 1)


def upper_rims(row):
    return shifted(row, "depth", 1)


def shards(
    pressure,
    vel_range,
    vel_depth,
    sound_speed,
    density,
    ahead_speed,
    ahead_density,
    shifts,
    sources,
    wavelet,
):
    height, breadth = pressure.shape
    at_end = lax.axis_index("range") == lax.axis_size("range") - 1
    at_bottom = lax.axis_index("depth") == lax.axis_size("depth") - 1
    col_start = lax.axis_index("range") * breadth
    row_start = lax.axis_index("depth") * height
    full_range = breadth * lax.axis_size("range")
    offset = jnp.int32(0)
    depth_onehot = (
        (sources[:, 0] - row_start)[:, None] == jnp.arange(height, dtype=jnp.int32)[None, :]
    ).astype(jnp.float32)
    extra = ahead_speed.shape[1]
    spread = breadth + extra
    zero_cols = jnp.zeros((height, extra), jnp.float32)
    pressure = jnp.concatenate([pressure, zero_cols], 1)
    vel_range = jnp.concatenate([vel_range, zero_cols], 1)
    vel_depth = jnp.concatenate([vel_depth, zero_cols], 1)
    sound_speed = jnp.concatenate([sound_speed, ahead_speed], 1)
    density = jnp.concatenate([density, ahead_density], 1)
    local_index = jnp.arange(spread, dtype=jnp.int32)
    abs_col = col_start + local_index
    usable = jnp.logical_or(at_end, local_index < breadth)
    inner_edge = jnp.logical_and(local_index == breadth - 1, jnp.logical_not(at_end))
    stiffness = density * sound_speed * sound_speed
    for segment in range(ITERS):
        live = jnp.logical_and(
            usable, jnp.logical_and(abs_col >= offset, abs_col < offset + full_range)
        )
        right_p, right_rho = right_rims(pressure, density)
        p_right = jnp.concatenate([pressure[:, 1:], jnp.zeros_like(pressure[:, :1])], 1)
        p_right = jnp.where(inner_edge[None, :], right_p, p_right)
        rho_right = jnp.concatenate([density[:, 1:], density[:, -1:]], 1)
        rho_right = jnp.where(inner_edge[None, :], right_rho, rho_right)
        rho_right = jnp.where((abs_col == offset + full_range - 1)[None, :], density, rho_right)
        fresh = vel_range - TIME_STEP * (2.0 / (density + rho_right)) * (p_right - pressure)
        vel_range = jnp.where(live[None, :], fresh, vel_range)
        lower_p, lower_rho = lower_rims(pressure, density)
        lower_rho = jnp.where(at_bottom, density[-1:], lower_rho)
        p_lower = jnp.concatenate([pressure[1:], lower_p], 0)
        rho_lower = jnp.concatenate([density[1:], lower_rho], 0)
        fresh = vel_depth - TIME_STEP * (2.0 / (density + rho_lower)) * (p_lower - pressure)
        vel_depth = jnp.where(live[None, :], fresh, vel_depth)
        left_edge = left_rims(vel_range[:, breadth - 1 : breadth])
        range_left = jnp.concatenate([left_edge, vel_range[:, :-1]], 1)
        range_left = jnp.where((abs_col == offset)[None, :], 0.0, range_left)
        upper_edge = upper_rims(vel_depth[-1:])
        depth_upper = jnp.concatenate([upper_edge, vel_depth[:-1]], 0)
        fresh = pressure - TIME_STEP * stiffness * (
            vel_range - range_left + (vel_depth - depth_upper)
        )
        amplitude = wavelet[:, segment]
        range_onehot = jnp.logical_and(
            sources[:, 1][:, None] == abs_col[None, :], usable[None, :]
        ).astype(jnp.float32)
        fresh = fresh + jnp.dot(
            (depth_onehot * amplitude[:, None]).T, range_onehot, precision=lax.Precision.HIGHEST
        )
        pressure = jnp.where(live[None, :], fresh, pressure)
        offset = offset + shifts[segment]
    tails = shifted((pressure[:, :extra], vel_range[:, :extra], vel_depth[:, :extra]), "range", -1)
    finals = []
    for field, tail in zip((pressure, vel_range, vel_depth), tails):
        after = jnp.where(at_end, field[:, breadth:], tail)
        joined = jnp.concatenate([field[:, :breadth], after], 1)
        finals.append(lax.dynamic_slice_in_dim(joined, offset, breadth, 1))
    return (finals[0], finals[1], finals[2])


def solution(mesh):
    placed = (
        P("depth", "range"),
        P("depth", "range"),
        P("depth", "range"),
        P("depth", "range"),
        P("depth", "range"),
        P("depth", None),
        P("depth", None),
        P(),
        P(),
        P(),
    )
    return jax.shard_map(
        shards,
        mesh=mesh,
        in_specs=placed,
        out_specs=(P("depth", "range"), P("depth", "range"), P("depth", "range")),
        check_vma=False,
    )
```

profile of v0, /device:TPU:43, one launch (start us, length us, event | category | flops | bytes accessed | tf_op | source)
XLA Modules:
  0.0 199.8 jit_solution(5306061344273016967)
XLA Ops:
  1.9 2.7 %collective-permute-start.4 = (f32[1,192]{0,1:T(8,128)S(1)}, f32[1,192]{0,1:T(8,128)}, u32[]{:S(2)}, u32[]{:S(2)}) collective-permute-start(f32[1,192]{0,1:T(8,128)S(1)} %pad_slice_fusion.4), channel_id=1, source_target_pairs={{1,0},{2,1},{3,2},{4,3},{5,4},{6,5},{7,6},{8,7},{9,8},{10,9},{11,1... | collective-permute-start | bytes 2312 | tf_op jit(solution)/shard_map/ppermute | solution.py:15
  5.9 2.7 %collective-permute-start.3 = (f32[1,192]{0,1:T(8,128)S(1)}, f32[1,192]{0,1:T(8,128)S(1)}, u32[]{:S(2)}, u32[]{:S(2)}) collective-permute-start(f32[1,192]{0,1:T(8,128)S(1)} %fusion.45), channel_id=1, source_target_pairs={{1,0},{2,1},{3,2},{4,3},{5,4},{6,5},{7,6},{8,7},{9,8},{10,9},{11,1... | collective-permute-start | bytes 2312 | tf_op jit(solution)/shard_map/ppermute | solution.py:15
  8.6 10.6 %collective-permute-start.1 = (f32[1024,1]{1,0:T(8,128)}, f32[1024,1]{1,0:T(8,128)}, u32[]{:S(2)}, u32[]{:S(2)}) collective-permute-start(f32[1024,1]{1,0:T(8,128)} %bitcast.19), channel_id=1, source_target_pairs={{16,0},{32,16},{48,32},{64,48},{80,64},{96,80},{112,96},{128,112},... | collective-permute-start | bytes 12296 | tf_op jit(solution)/shard_map/ppermute | solution.py:15
  30.9 3.1 %subtract_select_fusion.6 = (f32[1024,192]{0,1:T(8,128)S(1)}, f32[1024,192]{0,1:T(8,128)}, f32[1024,192]{0,1:T(8,128)}) fusion(f32[1024,128]{0,1:T(8,128)S(1)} %copy.21, f32[1,192]{0,1:T(8,128)} %collective-permute-done.4, f32[1023,192]{0,1:T(8,128)S(1)} %copy-done.16, f32[1024,128]{0,1:T(8,128)} %copy.25, pred[192]{0:T(512)(128)(4,1)S(1)} %and_and_fusion, ...), kind=kLoop, calls=%fused_computation.28 | loop fusion | flops 2752512 | bytes 6553792 | tf_op jit(solution)/shard_map/jit(_where)/select_n | solution.py:86
  34.0 5.1 %collective-permute-start.5 = (f32[1,192]{0,1:T(8,128)S(1)}, f32[1,192]{0,1:T(8,128)}, u32[]{:S(2)}, u32[]{:S(2)}) collective-permute-start(f32[1,192]{0,1:T(8,128)S(1)} %slice.259), channel_id=1, source_target_pairs={{0,1},{1,2},{2,3},{3,4},{4,5},{5,6},{6,7},{7,8},{8,9},{9,10},{10,1... | collective-permute-start | bytes 2312 | tf_op jit(solution)/shard_map/ppermute | solution.py:15
  49.3 6.1 %collective-permute-done.2 = f32[1024,1]{0,1:T(1,128)S(1)} collective-permute-done((f32[1024,1]{0,1:T(1,128)S(1)}, f32[1024,1]{0,1:T(1,128)S(1)}, u32[]{:S(2)}, u32[]{:S(2)}) %collective-permute-start.2) | collective-permute-done | bytes 4128 | tf_op jit(solution)/shard_map/ppermute | solution.py:15
  56.0 2.9 %fusion.3 = f32[1024,192]{0,1:T(8,128)S(1)} fusion(f32[1024,128]{0,1:T(8,128)S(1)} %copy.21, f32[1024,192]{0,1:T(8,128)} %get-tuple-element.17, f32[1024,192]{0,1:T(8,128)} %copy-done.11, f32[1024,191]{0,1:T(8,128)} %bitcast.33, f32[1024,1]{0,1:T(1,128)S(1)} %collective-permute-done.2, f32[1024,192]{0,1:T(8,128)} %copy-done.5, f32[1023,192]{0,1:T(8,128)} %bitcast.30, ...), kind=kOutput, calls=%fused_computation.12 | convolution fusion | flops 20859904 | bytes 5244320 | tf_op jit(solution)/shard_map/dot_general | solution.py:99
  59.0 6.1 %collective-permute-start.8 = (f32[1,192]{0,1:T(8,128)S(1)}, f32[1,192]{0,1:T(8,128)S(1)}, u32[]{:S(2)}, u32[]{:S(2)}) collective-permute-start(f32[1,192]{0,1:T(8,128)S(1)} %slice.266), channel_id=1, source_target_pairs={{1,0},{2,1},{3,2},{4,3},{5,4},{6,5},{7,6},{8,7},{9,8},{10,9},{11,1... | collective-permute-start | bytes 2312 | tf_op jit(solution)/shard_map/ppermute | solution.py:15
  65.0 3.6 %collective-permute-start.6 = (f32[1024,1]{0,1:T(1,128)S(1)}, f32[1024,1]{0,1:T(1,128)S(1)}, u32[]{:S(2)}, u32[]{:S(2)}) collective-permute-start(f32[1024,1]{0,1:T(1,128)S(1)} %slice.261), channel_id=1, source_target_pairs={{16,0},{32,16},{48,32},{64,48},{80,64},{96,80},{112,96},{128,112},... | collective-permute-start | bytes 12296 | tf_op jit(solution)/shard_map/ppermute | solution.py:15
  69.7 19.2 %collective-permute-done.8 = f32[1,192]{0,1:T(8,128)S(1)} collective-permute-done((f32[1,192]{0,1:T(8,128)S(1)}, f32[1,192]{0,1:T(8,128)S(1)}, u32[]{:S(2)}, u32[]{:S(2)}) %collective-permute-start.8) | collective-permute-done | bytes 800 | tf_op jit(solution)/shard_map/ppermute | solution.py:15
  94.2 5.9 %collective-permute-start.9 = (f32[1,192]{0,1:T(8,128)S(1)}, f32[1,192]{0,1:T(8,128)S(1)}, u32[]{:S(2)}, u32[]{:S(2)}) collective-permute-start(f32[1,192]{0,1:T(8,128)S(1)} %slice.267), channel_id=1, source_target_pairs={{0,1},{1,2},{2,3},{3,4},{4,5},{5,6},{6,7},{7,8},{8,9},{9,10},{10,1... | collective-permute-start | bytes 2312 | tf_op jit(solution)/shard_map/ppermute | solution.py:15
  101.9 2.9 %fusion.2 = f32[1024,192]{0,1:T(8,128)S(1)} fusion(f32[1024,192]{0,1:T(8,128)S(1)} %fusion.3, f32[1024,192]{0,1:T(8,128)} %get-tuple-element.17, f32[1024,192]{0,1:T(8,128)} %copy-done.9, f32[1024,191]{0,1:T(8,128)} %bitcast.32, f32[1024,1]{0,1:T(1,128)S(1)} %collective-permute-done.7, f32[1024,192]{0,1:T(8,128)} %get-tuple-element.15, ...), kind=kOutput, calls=%fused_computation.10 | convolution fusion | flops 20859904 | bytes 5506464 | tf_op jit(solution)/shard_map/dot_general | solution.py:99
  104.9 2.8 %collective-permute-start.12 = (f32[1,192]{0,1:T(8,128)S(1)}, f32[1,192]{0,1:T(8,128)S(1)}, u32[]{:S(2)}, u32[]{:S(2)}) collective-permute-start(f32[1,192]{0,1:T(8,128)S(1)} %slice.274), channel_id=1, source_target_pairs={{1,0},{2,1},{3,2},{4,3},{5,4},{6,5},{7,6},{8,7},{9,8},{10,9},{11,1... | collective-permute-start | bytes 2312 | tf_op jit(solution)/shard_map/ppermute | solution.py:15
  107.7 7.0 %collective-permute-start.10 = (f32[1024,1]{0,1:T(1,128)S(1)}, f32[1024,1]{0,1:T(1,128)S(1)}, u32[]{:S(2)}, u32[]{:S(2)}) collective-permute-start(f32[1024,1]{0,1:T(1,128)S(1)} %slice.269), channel_id=1, source_target_pairs={{16,0},{32,16},{48,32},{64,48},{80,64},{96,80},{112,96},{128,112},... | collective-permute-start | bytes 12296 | tf_op jit(solution)/shard_map/ppermute | solution.py:15
  116.4 2.6 %subtract_select_fusion.2 = (f32[1024,192]{0,1:T(8,128)}, f32[1024,192]{0,1:T(8,128)S(1)}) fusion(f32[1024,192]{0,1:T(8,128)} %get-tuple-element.15, f32[1024,192]{0,1:T(8,128)S(1)} %copy-done.14, f32[1024,192]{0,1:T(8,128)S(1)} %fusion.2, f32[1,192]{0,1:T(8,128)S(1)} %collective-permute-done.12, f32[1023,192]{0,1:T(8,128)S(1)} %slice.273, ...), kind=kLoop, calls=%fused_computation.22 | loop fusion | flops 3342336 | bytes 7868992 | tf_op jit(solution)/shard_map/jit(_where)/select_n | solution.py:86
  122.8 5.2 %collective-permute-start.13 = (f32[1,192]{0,1:T(8,128)S(1)}, f32[1,192]{0,1:T(8,128)S(1)}, u32[]{:S(2)}, u32[]{:S(2)}) collective-permute-start(f32[1,192]{0,1:T(8,128)S(1)} %slice.275), channel_id=1, source_target_pairs={{0,1},{1,2},{2,3},{3,4},{4,5},{5,6},{6,7},{7,8},{8,9},{9,10},{10,1... | collective-permute-start | bytes 2312 | tf_op jit(solution)/shard_map/ppermute | solution.py:15
  129.7 2.9 %fusion.1 = f32[1024,192]{0,1:T(8,128)S(1)} fusion(f32[1024,192]{0,1:T(8,128)S(1)} %fusion.2, f32[1024,192]{0,1:T(8,128)} %get-tuple-element.17, f32[1024,192]{0,1:T(8,128)} %copy-done.7, f32[1024,191]{0,1:T(8,128)} %bitcast.31, f32[1024,1]{0,1:T(1,128)S(1)} %collective-permute-done.11, f32[1024,192]{0,1:T(8,128)} %get-tuple-element.13, ...), kind=kOutput, calls=%fused_computation.8 | convolution fusion | flops 20859904 | bytes 5506464 | tf_op jit(solution)/shard_map/dot_general | solution.py:99
  132.6 2.2 %collective-permute-start.16 = (f32[1,192]{0,1:T(8,128)S(1)}, f32[1,192]{0,1:T(8,128)S(1)}, u32[]{:S(2)}, u32[]{:S(2)}) collective-permute-start(f32[1,192]{0,1:T(8,128)S(1)} %slice.282), channel_id=1, source_target_pairs={{1,0},{2,1},{3,2},{4,3},{5,4},{6,5},{7,6},{8,7},{9,8},{10,9},{11,1... | collective-permute-start | bytes 2312 | tf_op jit(solution)/shard_map/ppermute | solution.py:15
  134.8 7.6 %collective-permute-start.14 = (f32[1024,1]{0,1:T(1,128)S(1)}, f32[1024,1]{0,1:T(1,128)S(1)}, u32[]{:S(2)}, u32[]{:S(2)}) collective-permute-start(f32[1024,1]{0,1:T(1,128)S(1)} %slice.277), channel_id=1, source_target_pairs={{16,0},{32,16},{48,32},{64,48},{80,64},{96,80},{112,96},{128,112},... | collective-permute-start | bytes 12296 | tf_op jit(solution)/shard_map/ppermute | solution.py:15
  144.1 2.6 %subtract_select_fusion = (f32[1024,192]{0,1:T(8,128)S(1)}, f32[1024,192]{0,1:T(8,128)}) fusion(f32[1024,192]{0,1:T(8,128)} %get-tuple-element.13, f32[1024,192]{0,1:T(8,128)S(1)} %copy-done.15, f32[1024,192]{0,1:T(8,128)S(1)} %fusion.1, f32[1,192]{0,1:T(8,128)S(1)} %collective-permute-done.16, f32[1023,192]{0,1:T(8,128)S(1)} %slice.281, ...), kind=kLoop, calls=%fused_computation.19 | loop fusion | flops 3342336 | bytes 7868992 | tf_op jit(solution)/shard_map/jit(_where)/select_n | solution.py:86
  149.5 5.5 %collective-permute-start.17 = (f32[1,192]{0,1:T(8,128)S(1)}, f32[1,192]{0,1:T(8,128)S(1)}, u32[]{:S(2)}, u32[]{:S(2)}) collective-permute-start(f32[1,192]{0,1:T(8,128)S(1)} %slice.283), channel_id=1, source_target_pairs={{0,1},{1,2},{2,3},{3,4},{4,5},{5,6},{6,7},{7,8},{8,9},{9,10},{10,1... | collective-permute-start | bytes 2312 | tf_op jit(solution)/shard_map/ppermute | solution.py:15
  158.5 7.8 %collective-permute-start.19 = (f32[1024,64]{0,1:T(8,128)S(1)}, f32[1024,64]{0,1:T(8,128)S(1)}, u32[]{:S(2)}, u32[]{:S(2)}) collective-permute-start(f32[1024,64]{0,1:T(8,128)S(1)} %slice.290), channel_id=1, source_target_pairs={{16,0},{32,16},{48,32},{64,48},{80,64},{96,80},{112,96},{128,112},... | collective-permute-start | bytes 786440 | tf_op jit(solution)/shard_map/ppermute | solution.py:15
  166.3 3.5 %collective-permute-start.20 = (f32[1024,64]{0,1:T(8,128)}, f32[1024,64]{0,1:T(8,128)}, u32[]{:S(2)}, u32[]{:S(2)}) collective-permute-start(f32[1024,64]{0,1:T(8,128)} %slice.293), channel_id=1, source_target_pairs={{16,0},{32,16},{48,32},{64,48},{80,64},{96,80},{112,96},{128,112},... | collective-permute-start | bytes 786440 | tf_op jit(solution)/shard_map/ppermute | solution.py:15
  179.4 18.3 %collective-permute-done.18 = f32[1024,64]{0,1:T(8,128)} collective-permute-done((f32[1024,64]{0,1:T(8,128)}, f32[1024,64]{0,1:T(8,128)}, u32[]{:S(2)}, u32[]{:S(2)}) %collective-permute-start.18) | collective-permute-done | bytes 262176 | tf_op jit(solution)/shard_map/ppermute | solution.py:15
  (139 shorter events, 55.9 us)
Async XLA Ops:
  1.9 27.9 %collective-permute-start.4 = (f32[1,192]{0,1:T(8,128)S(1)}, f32[1,192]{0,1:T(8,128)}, u32[]{:S(2)}, u32[]{:S(2)}) collective-permute-start(f32[1,192]{0,1:T(8,128)S(1)} %pad_slice_fusion.4), channel_id=1, source_target_pairs={{1,0},{2,1},{3,2},{4,3},{5,4},{6,5},{7,6},{8,7},{9,8},{10,9},{11,1... | collective-permute-start | bytes 2312 | tf_op jit(solution)/shard_map/ppermute | solution.py:15
  5.9 23.8 %collective-permute-start.3 = (f32[1,192]{0,1:T(8,128)S(1)}, f32[1,192]{0,1:T(8,128)S(1)}, u32[]{:S(2)}, u32[]{:S(2)}) collective-permute-start(f32[1,192]{0,1:T(8,128)S(1)} %fusion.45), channel_id=1, source_target_pairs={{1,0},{2,1},{3,2},{4,3},{5,4},{6,5},{7,6},{8,7},{9,8},{10,9},{11,1... | collective-permute-start | bytes 2312 | tf_op jit(solution)/shard_map/ppermute | solution.py:15
  8.6 30.5 %collective-permute-start.1 = (f32[1024,1]{1,0:T(8,128)}, f32[1024,1]{1,0:T(8,128)}, u32[]{:S(2)}, u32[]{:S(2)}) collective-permute-start(f32[1024,1]{1,0:T(8,128)} %bitcast.19), channel_id=1, source_target_pairs={{16,0},{32,16},{48,32},{64,48},{80,64},{96,80},{112,96},{128,112},... | collective-permute-start | bytes 12296 | tf_op jit(solution)/shard_map/ppermute | solution.py:15
  19.2 23.3 %collective-permute-start = (f32[1024,1]{1,0:T(8,128)}, f32[1024,1]{1,0:T(8,128)}, u32[]{:S(2)}, u32[]{:S(2)}) collective-permute-start(f32[1024,1]{1,0:T(8,128)} %bitcast.20), channel_id=1, source_target_pairs={{16,0},{32,16},{48,32},{64,48},{80,64},{96,80},{112,96},{128,112},... | collective-permute-start | bytes 12296 | tf_op jit(solution)/shard_map/ppermute | solution.py:15
  24.7 64.2 %copy-start.1 = (f32[1024,191]{0,1:T(8,128)}, f32[1024,191]{0,1:T(8,128)S(1)}, u32[]{:S(2)}) copy-start(f32[1024,191]{0,1:T(8,128)S(1)} %get-tuple-element.35) | copy-start | bytes 2347012
  34.0 15.3 %collective-permute-start.5 = (f32[1,192]{0,1:T(8,128)S(1)}, f32[1,192]{0,1:T(8,128)}, u32[]{:S(2)}, u32[]{:S(2)}) collective-permute-start(f32[1,192]{0,1:T(8,128)S(1)} %slice.259), channel_id=1, source_target_pairs={{0,1},{1,2},{2,3},{3,4},{4,5},{5,6},{6,7},{7,8},{8,9},{9,10},{10,1... | collective-permute-start | bytes 2312 | tf_op jit(solution)/shard_map/ppermute | solution.py:15
  46.1 9.3 %collective-permute-start.2 = (f32[1024,1]{0,1:T(1,128)S(1)}, f32[1024,1]{0,1:T(1,128)S(1)}, u32[]{:S(2)}, u32[]{:S(2)}) collective-permute-start(f32[1024,1]{0,1:T(1,128)S(1)} %slice.251), channel_id=1, source_target_pairs={{0,16},{16,32},{32,48},{48,64},{64,80},{80,96},{96,112},{112,128},... | collective-permute-start | bytes 12296 | tf_op jit(solution)/shard_map/ppermute | solution.py:15
  59.0 29.9 %collective-permute-start.8 = (f32[1,192]{0,1:T(8,128)S(1)}, f32[1,192]{0,1:T(8,128)S(1)}, u32[]{:S(2)}, u32[]{:S(2)}) collective-permute-start(f32[1,192]{0,1:T(8,128)S(1)} %slice.266), channel_id=1, source_target_pairs={{1,0},{2,1},{3,2},{4,3},{5,4},{6,5},{7,6},{8,7},{9,8},{10,9},{11,1... | collective-permute-start | bytes 2312 | tf_op jit(solution)/shard_map/ppermute | solution.py:15
  65.0 23.9 %collective-permute-start.6 = (f32[1024,1]{0,1:T(1,128)S(1)}, f32[1024,1]{0,1:T(1,128)S(1)}, u32[]{:S(2)}, u32[]{:S(2)}) collective-permute-start(f32[1024,1]{0,1:T(1,128)S(1)} %slice.261), channel_id=1, source_target_pairs={{16,0},{32,16},{48,32},{64,48},{80,64},{96,80},{112,96},{128,112},... | collective-permute-start | bytes 12296 | tf_op jit(solution)/shard_map/ppermute | solution.py:15
  69.3 19.6 %copy-start.13 = (f32[1024,192]{0,1:T(8,128)S(1)}, f32[1024,192]{0,1:T(8,128)}, u32[]{:S(2)}) copy-start(f32[1024,192]{0,1:T(8,128)} %get-tuple-element.10) | copy-start | bytes 2359300
  69.6 19.3 %copy-start.12 = (f32[1024,192]{0,1:T(8,128)S(1)}, f32[1024,192]{0,1:T(8,128)}, u32[]{:S(2)}) copy-start(f32[1024,192]{0,1:T(8,128)} %copy-done.11) | copy-start | bytes 2359300
  91.3 10.6 %collective-permute-start.7 = (f32[1024,1]{0,1:T(1,128)S(1)}, f32[1024,1]{0,1:T(1,128)S(1)}, u32[]{:S(2)}, u32[]{:S(2)}) collective-permute-start(f32[1024,1]{0,1:T(1,128)S(1)} %slice.263), channel_id=1, source_target_pairs={{0,16},{16,32},{32,48},{48,64},{64,80},{80,96},{96,112},{112,128},... | collective-permute-start | bytes 12296 | tf_op jit(solution)/shard_map/ppermute | solution.py:15
  94.2 7.7 %collective-permute-start.9 = (f32[1,192]{0,1:T(8,128)S(1)}, f32[1,192]{0,1:T(8,128)S(1)}, u32[]{:S(2)}, u32[]{:S(2)}) collective-permute-start(f32[1,192]{0,1:T(8,128)S(1)} %slice.267), channel_id=1, source_target_pairs={{0,1},{1,2},{2,3},{3,4},{4,5},{5,6},{6,7},{7,8},{8,9},{9,10},{10,1... | collective-permute-start | bytes 2312 | tf_op jit(solution)/shard_map/ppermute | solution.py:15
  104.9 10.2 %collective-permute-start.12 = (f32[1,192]{0,1:T(8,128)S(1)}, f32[1,192]{0,1:T(8,128)S(1)}, u32[]{:S(2)}, u32[]{:S(2)}) collective-permute-start(f32[1,192]{0,1:T(8,128)S(1)} %slice.274), channel_id=1, source_target_pairs={{1,0},{2,1},{3,2},{4,3},{5,4},{6,5},{7,6},{8,7},{9,8},{10,9},{11,1... | collective-permute-start | bytes 2312 | tf_op jit(solution)/shard_map/ppermute | solution.py:15
  107.7 7.7 %collective-permute-start.10 = (f32[1024,1]{0,1:T(1,128)S(1)}, f32[1024,1]{0,1:T(1,128)S(1)}, u32[]{:S(2)}, u32[]{:S(2)}) collective-permute-start(f32[1024,1]{0,1:T(1,128)S(1)} %slice.269), channel_id=1, source_target_pairs={{16,0},{32,16},{48,32},{64,48},{80,64},{96,80},{112,96},{128,112},... | collective-permute-start | bytes 12296 | tf_op jit(solution)/shard_map/ppermute | solution.py:15
  119.9 9.8 %collective-permute-start.11 = (f32[1024,1]{0,1:T(1,128)S(1)}, f32[1024,1]{0,1:T(1,128)S(1)}, u32[]{:S(2)}, u32[]{:S(2)}) collective-permute-start(f32[1024,1]{0,1:T(1,128)S(1)} %slice.271), channel_id=1, source_target_pairs={{0,16},{16,32},{32,48},{48,64},{64,80},{80,96},{96,112},{112,128},... | collective-permute-start | bytes 12296 | tf_op jit(solution)/shard_map/ppermute | solution.py:15
  122.8 6.9 %collective-permute-start.13 = (f32[1,192]{0,1:T(8,128)S(1)}, f32[1,192]{0,1:T(8,128)S(1)}, u32[]{:S(2)}, u32[]{:S(2)}) collective-permute-start(f32[1,192]{0,1:T(8,128)S(1)} %slice.275), channel_id=1, source_target_pairs={{0,1},{1,2},{2,3},{3,4},{4,5},{5,6},{6,7},{7,8},{8,9},{9,10},{10,1... | collective-permute-start | bytes 2312 | tf_op jit(solution)/shard_map/ppermute | solution.py:15
  132.6 10.2 %collective-permute-start.16 = (f32[1,192]{0,1:T(8,128)S(1)}, f32[1,192]{0,1:T(8,128)S(1)}, u32[]{:S(2)}, u32[]{:S(2)}) collective-permute-start(f32[1,192]{0,1:T(8,128)S(1)} %slice.282), channel_id=1, source_target_pairs={{1,0},{2,1},{3,2},{4,3},{5,4},{6,5},{7,6},{8,7},{9,8},{10,9},{11,1... | collective-permute-start | bytes 2312 | tf_op jit(solution)/shard_map/ppermute | solution.py:15
  134.8 8.3 %collective-permute-start.14 = (f32[1024,1]{0,1:T(1,128)S(1)}, f32[1024,1]{0,1:T(1,128)S(1)}, u32[]{:S(2)}, u32[]{:S(2)}) collective-permute-start(f32[1024,1]{0,1:T(1,128)S(1)} %slice.277), channel_id=1, source_target_pairs={{16,0},{32,16},{48,32},{64,48},{80,64},{96,80},{112,96},{128,112},... | collective-permute-start | bytes 12296 | tf_op jit(solution)/shard_map/ppermute | solution.py:15
  147.5 22.4 %collective-permute-start.15 = (f32[1024,1]{0,1:T(1,128)S(1)}, f32[1024,1]{0,1:T(1,128)S(1)}, u32[]{:S(2)}, u32[]{:S(2)}) collective-permute-start(f32[1024,1]{0,1:T(1,128)S(1)} %slice.279), channel_id=1, source_target_pairs={{0,16},{16,32},{32,48},{48,64},{64,80},{80,96},{96,112},{112,128},... | collective-permute-start | bytes 12296 | tf_op jit(solution)/shard_map/ppermute | solution.py:15
  149.5 20.4 %collective-permute-start.17 = (f32[1,192]{0,1:T(8,128)S(1)}, f32[1,192]{0,1:T(8,128)S(1)}, u32[]{:S(2)}, u32[]{:S(2)}) collective-permute-start(f32[1,192]{0,1:T(8,128)S(1)} %slice.283), channel_id=1, source_target_pairs={{0,1},{1,2},{2,3},{3,4},{4,5},{5,6},{6,7},{7,8},{8,9},{9,10},{10,1... | collective-permute-start | bytes 2312 | tf_op jit(solution)/shard_map/ppermute | solution.py:15
  158.5 16.3 %collective-permute-start.19 = (f32[1024,64]{0,1:T(8,128)S(1)}, f32[1024,64]{0,1:T(8,128)S(1)}, u32[]{:S(2)}, u32[]{:S(2)}) collective-permute-start(f32[1024,64]{0,1:T(8,128)S(1)} %slice.290), channel_id=1, source_target_pairs={{16,0},{32,16},{48,32},{64,48},{80,64},{96,80},{112,96},{128,112},... | collective-permute-start | bytes 786440 | tf_op jit(solution)/shard_map/ppermute | solution.py:15
  166.3 11.0 %collective-permute-start.20 = (f32[1024,64]{0,1:T(8,128)}, f32[1024,64]{0,1:T(8,128)}, u32[]{:S(2)}, u32[]{:S(2)}) collective-permute-start(f32[1024,64]{0,1:T(8,128)} %slice.293), channel_id=1, source_target_pairs={{16,0},{32,16},{48,32},{64,48},{80,64},{96,80},{112,96},{128,112},... | collective-permute-start | bytes 786440 | tf_op jit(solution)/shard_map/ppermute | solution.py:15
  172.8 24.9 %collective-permute-start.18 = (f32[1024,64]{0,1:T(8,128)}, f32[1024,64]{0,1:T(8,128)}, u32[]{:S(2)}, u32[]{:S(2)}) collective-permute-start(f32[1024,64]{0,1:T(8,128)} %slice.287), channel_id=1, source_target_pairs={{16,0},{32,16},{48,32},{64,48},{80,64},{96,80},{112,96},{128,112},... | collective-permute-start | bytes 786440 | tf_op jit(solution)/shard_map/ppermute | solution.py:15
  (22 other events, 67.6 us)
where the time goes:
time: 202 us; the launch traced here: 200 us
  starting transfers between devices  90 us (45%)
  waiting for transfers between devices  47.7 us (24%)
  local copies, waits for them, and re-layouts  24.8 us (12%)
  other arithmetic  21.3 us (11%)
  matrix products  10.8 us (5%)
  between operations  5.15 us (3%)
    ppermute x21, starting transfers between devices, shifted(): return lax.ppermute(shard, axis, pairs)  90 us
    ppermute x21, waiting for transfers between devices, shifted(): return lax.ppermute(shard, axis, pairs)  47.7 us
    unnamed x58, local copies, waits for them, and re-layouts  14.8 us
    dot_general x4, matrix products, shards(): jnp.dot((depth_onehot * amplitude[:, None]).T, range_onehot, precision=la...  10.8 us
    select_n x4, other arithmetic, shards(): vel_depth = jnp.where(live[None, :], fresh, vel_depth)  9.73 us
  transfers between devices with their start and end apart: 21, of which 8 were waited for; matrix products, arithmetic and copies ran while one was open for 15% of the time, Pallas kernels for 0%

commit v1 on v0

v1 whole, which is shorter than its diff:
```python
import functools

import jax
import jax.numpy as jnp
from jax import lax
from jax.experimental import pallas as pl
from jax.experimental.pallas import tpu as pltpu
from jax.sharding import PartitionSpec as P

ITERS = 4
TIME_STEP = 0.6
MESH = pl.DeviceIdType.MESH
HALO = 8
ROWS = 128
TAIL = 64


def advance(fields, row, col, offsets, points, full, left, ends):
    p, vr, vz, c, rho = fields
    n = p.shape[0]
    a = (2.0 * TIME_STEP) / (rho + pltpu.roll(rho, 127, 1))
    b = (2.0 * TIME_STEP) / (rho + pltpu.roll(rho, n - 1, 0))
    b = jnp.where(row >= 0, b, 0.0)
    k = TIME_STEP * (rho * c * c)
    if ends:
        a_last = TIME_STEP / rho
    masks = []
    for where_row, where_col, _ in points:
        masks.append(jnp.logical_and(row == where_row, col == where_col))
    for t in range(ITERS):
        push_r = pltpu.roll(p, 127, 1) - p
        push_z = b * (pltpu.roll(p, n - 1, 0) - p)
        if ends:
            on = col < full + offsets[t]
            push_r = jnp.where(col == full + offsets[t] - 1, a_last, a) * push_r
            vr = jnp.where(on, vr - push_r, vr)
            vz = jnp.where(on, vz - push_z, vz)
        else:
            vr = vr - a * push_r
            vz = vz - push_z
        back = pltpu.roll(vr, 1, 1)
        if left:
            back = jnp.where(col == offsets[t], 0.0, back)
        fresh = p - k * ((vr - back) + (vz - pltpu.roll(vz, 1, 0)))
        if ends:
            fresh = jnp.where(on, fresh, p)
        p = fresh
        for mask, (_, _, amounts) in zip(masks, points):
            p = p + jnp.where(mask, amounts[t], 0.0)
    return p, vr, vz


def pack_columns(load, lane, start, place):
    total = None
    for g in range(8):
        moved = pltpu.roll(load(g), (16 * g + place - start) % 128, 1)
        total = moved if total is None else jnp.where(lane >= 16 * g + place, moved, total)
    return total


def kernel(
    n_range, n_depth,
    p_in, vr_in, vz_in, c_in, rho_in, ac_in, ad_in, shifts, sources, wavelet,
    main, tail, strip,
    ext, beyond, raw, tail_out, edge_out, edge_in,
    in_sem, raw_sem, halo_send, halo_recv, far_send, far_recv, edge_send, edge_recv, tail_send, tail_recv,
):
    r = lax.axis_index("range")
    d = lax.axis_index("depth")
    height = p_in.shape[0]
    chunks = height // ROWS
    at_end = r == n_range - 1
    full = 128 * n_range
    span = ROWS + 2 * HALO

    barrier = pltpu.get_barrier_semaphore()

    @pl.when(r < n_range - 1)
    def _():
        pl.semaphore_signal(barrier, inc=1, device_id={"range": r + 1}, device_id_type=MESH)

    @pl.when(d > 0)
    def _():
        pl.semaphore_signal(barrier, inc=1, device_id={"depth": d - 1}, device_id_type=MESH)

    @pl.when(d < n_depth - 1)
    def _():
        pl.semaphore_signal(barrier, inc=1, device_id={"depth": d + 1}, device_id_type=MESH)

    loads = [
        pltpu.make_async_copy(ref, ext.at[i, pl.ds(HALO, height)], in_sem.at[i])
        for i, ref in enumerate((p_in, vr_in, vz_in, c_in, rho_in))
    ]
    for copy in loads:
        copy.start()
    far_loads = [
        pltpu.make_async_copy(ref, raw.at[i], raw_sem.at[i]) for i, ref in enumerate((ac_in, ad_in))
    ]

    @pl.when(at_end)
    def _():
        for copy in far_loads:
            copy.start()

    offsets = [jnp.int32(0)]
    for t in range(ITERS - 1):
        offsets.append(offsets[-1] + shifts[t])
    points = [
        (sources[i, 0], sources[i, 1], [wavelet[i, t] for t in range(ITERS)])
        for i in range(sources.shape[0])
    ]
    row_start = d * height
    iota_row = lax.broadcasted_iota(jnp.int32, (span, 128), 0)
    lane = lax.broadcasted_iota(jnp.int32, (span, 128), 1)
    col = lane + 128 * r

    for copy in loads:
        copy.wait()

    def pack_tail(i, results, target):
        half = ROWS // 2
        low = lane[:half] < TAIL
        for f, value in enumerate(results):
            first = value[HALO : HALO + half]
            second = pltpu.roll(value[HALO + half : HALO + ROWS], TAIL, 1)
            target[i, f] = jnp.where(low, first, second)

    def main_chunk(i):
        at = pl.multiple_of(i * ROWS, ROWS)
        fields = [ext[f, pl.ds(at, span)] for f in range(5)]
        row = iota_row + (row_start - HALO + at)
        results = advance(fields, row, col, offsets, points, full, True, False)
        for f, value in enumerate(results):
            main[f, pl.ds(at, ROWS)] = value[HALO : HALO + ROWS]
        pack_tail(i, results, tail_out)

    def tail_copy(i):
        return pltpu.make_async_remote_copy(
            src_ref=tail_out.at[i], dst_ref=tail.at[i],
            send_sem=tail_send.at[i], recv_sem=tail_recv.at[i],
            device_id={"range": r - 1}, device_id_type=MESH,
        )

    def send_tail(i):
        @pl.when(r > 0)
        def _():
            tail_copy(i).start()

    pl.semaphore_wait(
        barrier, jnp.minimum(r, 1) + jnp.minimum(d, 1) + jnp.minimum(n_depth - 1 - d, 1)
    )

    up = pltpu.make_async_remote_copy(
        src_ref=ext.at[:, pl.ds(HALO, HALO)], dst_ref=ext.at[:, pl.ds(HALO + height, HALO)],
        send_sem=halo_send.at[0], recv_sem=halo_recv.at[0],
        device_id={"depth": d - 1}, device_id_type=MESH,
    )
    down = pltpu.make_async_remote_copy(
        src_ref=ext.at[:, pl.ds(height, HALO)], dst_ref=ext.at[:, pl.ds(0, HALO)],
        send_sem=halo_send.at[1], recv_sem=halo_recv.at[1],
        device_id={"depth": d + 1}, device_id_type=MESH,
    )

    @pl.when(d > 0)
    def _():
        up.start()

    @pl.when(d < n_depth - 1)
    def _():
        down.start()

    zeros = jnp.zeros((HALO, 128), jnp.float32)

    @pl.when(d == 0)
    def _():
        for f in range(4):
            ext[f, pl.ds(0, HALO)] = zeros
        ext[4, pl.ds(0, HALO)] = zeros + 1.0

    @pl.when(d == n_depth - 1)
    def _():
        for f in range(4):
            ext[f, pl.ds(HALO + height, HALO)] = zeros
        last = ext[4, pl.ds(height, HALO)]
        ext[4, pl.ds(HALO + height, HALO)] = jnp.broadcast_to(last[HALO - 1 :], (HALO, 128))

    def interior(i, carry):
        main_chunk(i)
        send_tail(i)
        return carry

    lax.fori_loop(1, chunks - 1, interior, 0)

    @pl.when(d < n_depth - 1)
    def _():
        up.wait_recv()

    @pl.when(d > 0)
    def _():
        down.wait_recv()

    def rim(i, carry):
        main_chunk(i * (chunks - 1))
        send_tail(i * (chunks - 1))
        return carry

    lax.fori_loop(0, 2, rim, 0)

    fold = span // 2
    high = (lane % 16) >= 8
    edge_copy = pltpu.make_async_remote_copy(
        src_ref=edge_out, dst_ref=edge_in, send_sem=edge_send, recv_sem=edge_recv,
        device_id={"range": r - 1}, device_id_type=MESH,
    )

    @pl.when(r > 0)
    def _():
        for f in range(5):
            packed = pack_columns(lambda g: ext[f, pl.ds(g * ROWS, span)], lane, 0, 8)
            edge_out[f] = jnp.where(
                high[:fold], packed[:fold], pltpu.roll(packed[fold:], 120, 1)
            )
        edge_copy.start()

    @pl.when(at_end)
    def _():
        for copy in far_loads:
            copy.wait()
        for f, fill in enumerate((0.0, 1.0)):
            side = jnp.full((height, 64), fill, jnp.float32)
            beyond[f, pl.ds(HALO, height)] = jnp.concatenate([raw[f], side], 1)

        far_up = pltpu.make_async_remote_copy(
            src_ref=beyond.at[:, pl.ds(HALO, HALO)], dst_ref=beyond.at[:, pl.ds(HALO + height, HALO)],
            send_sem=far_send.at[0], recv_sem=far_recv.at[0],
            device_id={"depth": d - 1}, device_id_type=MESH,
        )
        far_down = pltpu.make_async_remote_copy(
            src_ref=beyond.at[:, pl.ds(height, HALO)], dst_ref=beyond.at[:, pl.ds(0, HALO)],
            send_sem=far_send.at[1], recv_sem=far_recv.at[1],
            device_id={"depth": d + 1}, device_id_type=MESH,
        )

        @pl.when(d > 0)
        def _():
            far_up.start()

        @pl.when(d < n_depth - 1)
        def _():
            far_down.start()

        @pl.when(d == 0)
        def _():
            beyond[0, pl.ds(0, HALO)] = zeros
            beyond[1, pl.ds(0, HALO)] = zeros + 1.0

        @pl.when(d == n_depth - 1)
        def _():
            beyond[0, pl.ds(HALO + height, HALO)] = zeros
            last = beyond[1, pl.ds(height, HALO)]
            beyond[1, pl.ds(HALO + height, HALO)] = jnp.broadcast_to(last[HALO - 1 :], (HALO, 128))

        @pl.when(d < n_depth - 1)
        def _():
            far_up.wait_recv()

        @pl.when(d > 0)
        def _():
            far_down.wait_recv()

        nothing = jnp.zeros((span, 128), jnp.float32)

        def far_chunk(i, carry):
            at = pl.multiple_of(i * ROWS, ROWS)
            fields = [nothing] * 3 + [beyond[f, pl.ds(at, span)] for f in range(2)]
            row = iota_row + (row_start - HALO + at)
            results = advance(fields, row, lane + full, offsets, [], full, False, True)
            pack_tail(i, results, tail)
            return carry

        lax.fori_loop(0, chunks, far_chunk, 0)
        for f in range(3):
            edge_in[f] = nothing[:fold]
        for f in range(2):
            packed = pack_columns(lambda g: beyond[f, pl.ds(g * ROWS, span)], lane, 0, 8)
            edge_in[3 + f] = jnp.where(
                high[:fold], packed[:fold], pltpu.roll(packed[fold:], 120, 1)
            )

        @pl.when(d > 0)
        def _():
            far_up.wait_send()

        @pl.when(d < n_depth - 1)
        def _():
            far_down.wait_send()

    own = [
        pack_columns(lambda g: ext[f, pl.ds(g * ROWS, span)], lane, 120, 0) for f in range(5)
    ]

    @pl.when(r < n_range - 1)
    def _():
        edge_copy.wait_recv()

    fields = []
    for f in range(5):
        folded = edge_in[f]
        other = jnp.concatenate([folded, pltpu.roll(folded, 8, 1)], 0)
        fields.append(jnp.where(high, other, own[f]))
    row = iota_row + (row_start - HALO) + ROWS * (lane // 16)
    results = advance(
        fields, row, 128 * r + 120 + lane % 16, offsets, points, full, False, True
    )
    for f, value in enumerate(results):
        strip[f] = value[HALO : HALO + ROWS]

    @pl.when(r < n_range - 1)
    def _():
        for i in range(chunks):
            tail_copy(i).wait_recv()

    @pl.when(r > 0)
    def _():
        edge_copy.wait_send()
        for i in range(chunks):
            tail_copy(i).wait_send()

    @pl.when(d > 0)
    def _():
        up.wait_send()

    @pl.when(d < n_depth - 1)
    def _():
        down.wait_send()


def finish(main, tail, strip, shifts, p_out, vr_out, vz_out, out, sem):
    chunks = tail.shape[0]
    offset = shifts[0]
    for t in range(1, ITERS):
        offset = offset + shifts[t]
    half = ROWS // 2
    lane = lax.broadcasted_iota(jnp.int32, (half, 128), 1)
    copies = []
    for i in range(chunks):
        for f, target in enumerate((p_out, vr_out, vz_out)):
            packed = tail[i, f]
            for h in range(2):
                at = i * ROWS + h * half
                edge = pltpu.roll(strip[f, h * half : (h + 1) * half], (120 - 16 * i) % 128, 1)
                near = jnp.where(lane >= 124, edge, main[f, at : at + half])
                far = packed if h == 0 else pltpu.roll(packed, TAIL, 1)
                far = jnp.where(lane < 4, edge, far)
                out[f, at : at + half] = pltpu.roll(
                    jnp.where(lane >= offset, near, far), 128 - offset, 1
                )
            copy = pltpu.make_async_copy(
                out.at[f, pl.ds(i * ROWS, ROWS)], target.at[pl.ds(i * ROWS, ROWS)], sem.at[i, f]
            )
            copy.start()
            copies.append(copy)
    for copy in copies:
        copy.wait()


def solution(mesh):
    n_range, n_depth = mesh.shape["range"], mesh.shape["depth"]

    def step(p, vr, vz, c, rho, ac, ad, shifts, sources, wavelet):
        height = p.shape[0]
        chunks = height // ROWS
        span = ROWS + 2 * HALO
        f32 = jnp.float32
        dma = pltpu.SemaphoreType.DMA
        any_space = pl.BlockSpec(memory_space=pl.ANY)
        vmem = pl.BlockSpec(memory_space=pltpu.VMEM)
        smem = pl.BlockSpec(memory_space=pltpu.SMEM)
        main, tail, strip = pl.pallas_call(
            functools.partial(kernel, n_range, n_depth),
            out_shape=(
                jax.ShapeDtypeStruct((3, height, 128), f32),
                jax.ShapeDtypeStruct((chunks, 3, ROWS // 2, 128), f32),
                jax.ShapeDtypeStruct((3, ROWS, 128), f32),
            ),
            in_specs=[any_space] * 7 + [smem] * 3,
            out_specs=(vmem, vmem, vmem),
            scratch_shapes=[
                pltpu.VMEM((5, height + 2 * HALO, 128), f32),
                pltpu.VMEM((2, height + 2 * HALO, 128), f32),
                pltpu.VMEM((2, height, 64), f32),
                pltpu.VMEM((chunks, 3, ROWS // 2, 128), f32),
                pltpu.VMEM((5, span // 2, 128), f32),
                pltpu.VMEM((5, span // 2, 128), f32),
                dma((5,)), dma((2,)), dma((2,)), dma((2,)), dma((2,)), dma((2,)),
                dma, dma, dma((chunks,)), dma((chunks,)),
            ],
            compiler_params=pltpu.CompilerParams(
                collective_id=1, has_side_effects=True, vmem_limit_bytes=32 * 2**20
            ),
        )(p, vr, vz, c, rho, ac, ad, shifts, sources, wavelet)
        block = jax.ShapeDtypeStruct((height, 128), f32)
        return pl.pallas_call(
            finish,
            out_shape=(block, block, block),
            in_specs=[vmem, vmem, vmem, smem],
            out_specs=(any_space, any_space, any_space),
            scratch_shapes=[pltpu.VMEM((3, height, 128), f32), dma((chunks, 3))],
            compiler_params=pltpu.CompilerParams(vmem_limit_bytes=16 * 2**20),
        )(main, tail, strip, shifts)

    block = P("depth", "range")
    return jax.shard_map(
        step,
        mesh=mesh,
        in_specs=(block,) * 5 + (P("depth", None),) * 2 + (P(),) * 3,
        out_specs=(block, block, block),
        check_vma=False,
    )
```

time: 202 us -> 66.7 us (0.33)
  the two profiles are of different devices: /device:TPU:43 before, /device:TPU:54 now
where the time goes in v1:
time: 66.7 us; the launch traced here: 66.4 us
  Pallas kernels  59.7 us (90%)
  local copies, waits for them, and re-layouts  6.01 us (9%)
  between operations  0.73 us (1%)
    pallas_call x1, Pallas kernels, step(): pl.pallas_call(functools.partial(kernel, n_range, n_depth), out_shape=(ja...  54.6 us
    unnamed x16, local copies, waits for them, and re-layouts  6.01 us
    pallas_call x1, Pallas kernels, step(): pl.pallas_call(finish, out_shape=(block, block, block), in_specs=[vmem, v...  5.06 us

profile of v1, /device:TPU:54, one launch (start us, length us, event | category | flops | bytes accessed | tf_op | source)
XLA Modules:
  0.0 66.4 jit_solution(18347476913083897813)
XLA Ops:
  0.6 0.0 copy-start.5
  0.6 0.0 copy-start.2
  0.7 0.0 copy-start.1
  0.7 0.0 copy-start
  0.7 0.9 %copy.15.sources = s32[8,2]{1,0:T(8,128)S(1)} copy(s32[8,2]{0,1:T(2,128)} %param.18) | data formatting | bytes 128 | tf_op args[8]
  1.5 0.8 %copy.16.wavelet = f32[8,4]{1,0:T(8,128)S(1)} copy(f32[8,4]{0,1:T(4,128)} %param.19) | data formatting | bytes 256 | tf_op args[9]
  2.3 1.1 %copy.13.ac_in = f32[1024,64]{1,0:T(8,128)S(1)} copy(f32[1024,64]{0,1:T(8,128)} %param.15) | data formatting | bytes 524288 | tf_op args[5]
  3.4 1.1 %copy.14.ad_in = f32[1024,64]{1,0:T(8,128)S(1)} copy(f32[1024,64]{0,1:T(8,128)} %param.16) | data formatting | bytes 524288 | tf_op args[6]
  4.6 0.0 copy-done.5
  4.6 0.0 copy-done.2
  4.6 0.0 copy-done.1
  4.6 0.0 copy-done
  4.6 0.0 copy-start.3
  4.7 1.0 %copy-done.3 = f32[1024,128]{1,0:T(8,128)S(1)} copy-done((f32[1024,128]{1,0:T(8,128)S(1)}, f32[1024,128]{1,0:T(8,128)}, u32[]{:S(2)}) %copy-start.3) | copy-done | bytes 524312
  5.7 0.0 copy-start.4
  5.7 1.0 %copy-done.4 = f32[1024,128]{1,0:T(8,128)S(1)} copy-done((f32[1024,128]{1,0:T(8,128)S(1)}, f32[1024,128]{1,0:T(8,128)}, u32[]{:S(2)}) %copy-start.4) | copy-done | bytes 524312
  6.7 54.6 %shard_map.121 = (f32[3,1024,128]{2,1,0:T(8,128)S(1)}, f32[8,3,64,128]{3,2,1,0:T(8,128)S(1)}, f32[3,128,128]{2,1,0:T(8,128)S(1)}) custom-call(f32[1024,128]{1,0:T(8,128)S(1)} %copy-done, f32[1024,128]{1,0:T(8,128)S(1)} %copy-done.1, f32[1024,128]{1,0:T(8,128)S(1)} %copy-done.2, f32[1024,128]{1,0:T(8,128)S(1)} %copy-done.3, f32[1024,128]{1,0:T(8,128)S(1)} %copy-done.4, ...), custom_call_target="tpu_custom_call" | custom-call | tf_op jit(solution)/shard_map/pallas_call | solution.py:379
  61.4 5.1 %shard_map.122 = (f32[1024,128]{1,0:T(8,128)}, f32[1024,128]{1,0:T(8,128)}, f32[1024,128]{1,0:T(8,128)}) custom-call(f32[3,1024,128]{2,1,0:T(8,128)S(1)} %get-tuple-element.6.main, f32[8,3,64,128]{3,2,1,0:T(8,128)S(1)} %get-tuple-element.7.tail, f32[3,128,128]{2,1,0:T(8,128)S(1)} %get-tuple-element.8.strip, s32[4]{0:T(128)S(1)} %copy-done.5), custom_call_target="tpu_custom_call" | custom-call | tf_op jit(solution)/shard_map/pallas_call | solution.py:403
Async XLA Ops:
  0.6 4.0 %copy-start.5 = (s32[4]{0:T(128)S(1)}, s32[4]{0:T(128)}, u32[]{:S(2)}) copy-start(s32[4]{0:T(128)} %shifts.3) | copy-start | bytes 52
  0.6 4.0 %copy-start.2 = (f32[1024,128]{1,0:T(8,128)S(1)}, f32[1024,128]{1,0:T(8,128)}, u32[]{:S(2)}) copy-start(f32[1024,128]{1,0:T(8,128)} %vz_in.1) | copy-start | bytes 1572868
  0.7 4.0 %copy-start.1 = (f32[1024,128]{1,0:T(8,128)S(1)}, f32[1024,128]{1,0:T(8,128)}, u32[]{:S(2)}) copy-start(f32[1024,128]{1,0:T(8,128)} %vr_in.1) | copy-start | bytes 1572868
  0.7 4.0 %copy-start = (f32[1024,128]{1,0:T(8,128)S(1)}, f32[1024,128]{1,0:T(8,128)}, u32[]{:S(2)}) copy-start(f32[1024,128]{1,0:T(8,128)} %p_in.1) | copy-start | bytes 1572868
  4.6 1.0 %copy-start.3 = (f32[1024,128]{1,0:T(8,128)S(1)}, f32[1024,128]{1,0:T(8,128)}, u32[]{:S(2)}) copy-start(f32[1024,128]{1,0:T(8,128)} %c_in.1) | copy-start | bytes 1572868
  5.7 1.0 %copy-start.4 = (f32[1024,128]{1,0:T(8,128)S(1)}, f32[1024,128]{1,0:T(8,128)}, u32[]{:S(2)}) copy-start(f32[1024,128]{1,0:T(8,128)} %rho_in.1) | copy-start | bytes 1572868

commit v2 on v1

v2 whole, which is shorter than its diff:
```python
import functools

import jax
import jax.numpy as jnp
from jax import lax
from jax.experimental import pallas as pl
from jax.experimental.pallas import tpu as pltpu
from jax.sharding import PartitionSpec as P

ITERS = 4
TIME_STEP = 0.6
MESH = pl.DeviceIdType.MESH
HALO = 8
ROWS = 128
TAIL = 64
RING = 8
FAR = 5


def advance(fields, row, col, offsets, points, full, left, ends):
    p, vr, vz, c, rho = fields
    n = p.shape[0]
    a = (2.0 * TIME_STEP) / (rho + pltpu.roll(rho, 127, 1))
    b = (2.0 * TIME_STEP) / (rho + pltpu.roll(rho, n - 1, 0))
    b = jnp.where(row >= 0, b, 0.0)
    k = TIME_STEP * (rho * c * c)
    if ends:
        a_last = TIME_STEP / rho
    masks = []
    for where_row, where_col, _ in points:
        masks.append(jnp.logical_and(row == where_row, col == where_col))
    for t in range(ITERS):
        push_r = pltpu.roll(p, 127, 1) - p
        push_z = b * (pltpu.roll(p, n - 1, 0) - p)
        if ends:
            on = col < full + offsets[t]
            push_r = jnp.where(col == full + offsets[t] - 1, a_last, a) * push_r
            vr = jnp.where(on, vr - push_r, vr)
            vz = jnp.where(on, vz - push_z, vz)
        else:
            vr = vr - a * push_r
            vz = vz - push_z
        back = pltpu.roll(vr, 1, 1)
        if left:
            back = jnp.where(col == offsets[t], 0.0, back)
        fresh = p - k * ((vr - back) + (vz - pltpu.roll(vz, 1, 0)))
        if ends:
            fresh = jnp.where(on, fresh, p)
        p = fresh
        for mask, (_, _, amounts) in zip(masks, points):
            p = p + jnp.where(mask, amounts[t], 0.0)
    return p, vr, vz


def pack_columns(load, lane, start, place):
    total = None
    for g in range(8):
        moved = pltpu.roll(load(g), (16 * g + place - start) % 128, 1)
        total = moved if total is None else jnp.where(lane >= 16 * g + place, moved, total)
    return total


def kernel(
    n_range, n_depth,
    p_in, vr_in, vz_in, c_in, rho_in, ac_in, ad_in, shifts, sources, wavelet,
    main, tail, strip,
    ext, beyond, raw, tail_out, edge_out, edge_in, relay, relay_edge, seam, main_out, strip_out,
    in_sem, raw_sem, halo_send, halo_recv, far_send, far_recv, edge_send, edge_recv, tail_send, tail_recv,
    pass_send, pass_recv, edge_pass_send, edge_pass_recv, ready_wrap, ready_next, main_sem, strip_sem,
):
    r = lax.axis_index("range")
    d = lax.axis_index("depth")
    z = lax.rem(r, RING)
    height = p_in.shape[0]
    chunks = height // ROWS
    at_end = r == n_range - 1
    full = 128 * n_range
    span = ROWS + 2 * HALO
    half = ROWS // 2
    quarter = ROWS // 4

    seam_out = jnp.logical_and(z == 0, r > 0)
    seam_in = jnp.logical_and(z == RING - 1, r < n_range - 1)
    upper = r >= RING
    lower = r < n_range - RING
    base = jnp.logical_and(z == 0, lower)
    first_stop = jnp.logical_and(jnp.logical_and(z >= 1, z <= 3), upper)
    second_stop = jnp.logical_and(jnp.logical_and(z >= 4, z <= 6), lower)
    plain_out = z > 0
    plain_in = z < RING - 1

    def one(flag):
        return jnp.where(flag, 1, 0)

    barrier = pltpu.get_barrier_semaphore()

    def greet(flag, semaphore, **where):
        @pl.when(flag)
        def _():
            pl.semaphore_signal(semaphore, inc=1, device_id=where, device_id_type=MESH)

    greet(plain_in, barrier, range=r + 1)
    greet(base, barrier, range=r + RING)
    greet(base, barrier, range=r + RING - 1)
    greet(seam_out, barrier, range=r + 2)
    greet(seam_out, barrier, range=r + 3)
    greet(first_stop, barrier, range=r - RING + 3)
    greet(jnp.logical_and(z == 4, lower), barrier, range=r + 3)
    greet(jnp.logical_and(z == 5, lower), barrier, range=r + 2)
    greet(d > 0, barrier, depth=d - 1)
    greet(d < n_depth - 1, barrier, depth=d + 1)

    loads = [
        pltpu.make_async_copy(ref, ext.at[i, pl.ds(HALO, height)], in_sem.at[i])
        for i, ref in enumerate((p_in, vr_in, vz_in, c_in, rho_in))
    ]
    for copy in loads:
        copy.start()
    far_loads = [
        pltpu.make_async_copy(ref, raw.at[i], raw_sem.at[i]) for i, ref in enumerate((ac_in, ad_in))
    ]

    @pl.when(at_end)
    def _():
        for copy in far_loads:
            copy.start()

    offsets = [jnp.int32(0)]
    for t in range(ITERS - 1):
        offsets.append(offsets[-1] + shifts[t])
    points = [
        (sources[0, i], sources[1, i], [wavelet[t, i] for t in range(ITERS)])
        for i in range(sources.shape[1])
    ]
    row_start = d * height
    iota_row = lax.broadcasted_iota(jnp.int32, (span, 128), 0)
    lane = lax.broadcasted_iota(jnp.int32, (span, 128), 1)
    col = lane + 128 * r

    for copy in loads:
        copy.wait()

    def pack_tail(i, results, target):
        low = lane[:half] < TAIL
        for f, value in enumerate(results):
            first = value[HALO : HALO + half]
            second = pltpu.roll(value[HALO + half : HALO + ROWS], TAIL, 1)
            target[i, f] = jnp.where(low, first, second)

    def main_copy(i):
        at = pl.ds(pl.multiple_of(i * ROWS, ROWS), ROWS)
        return pltpu.make_async_copy(main_out.at[:, at], main.at[:, at], main_sem.at[i])

    def main_chunk(i):
        at = pl.multiple_of(i * ROWS, ROWS)
        fields = [ext[f, pl.ds(at, span)] for f in range(5)]
        row = iota_row + (row_start - HALO + at)
        results = advance(fields, row, col, offsets, points, full, True, False)
        for f, value in enumerate(results):
            main_out[f, pl.ds(at, ROWS)] = value[HALO : HALO + ROWS]
        pack_tail(i, results, tail_out)
        main_copy(i).start()

    def remote(src, dst, send, recv, **where):
        return pltpu.make_async_remote_copy(
            src_ref=src, dst_ref=dst, send_sem=send, recv_sem=recv,
            device_id=where, device_id_type=MESH,
        )

    def tail_copy(i):
        return remote(tail_out.at[i], tail.at[i], tail_send.at[i], tail_recv.at[i], range=r - 1)

    def low_copy(i):
        return remote(tail_out.at[i], relay.at[i], tail_send.at[i], pass_recv.at[i, 0], range=r - RING)

    def wrap_copy(i):
        return remote(relay.at[i], tail.at[i], pass_send.at[i, 0], tail_recv.at[i], range=r + RING - 1)

    def part(ref, i, j):
        return ref.at[i, :, pl.ds(j * quarter, quarter)]

    def hop(i, j, source, target, to):
        return remote(part(source, i, j), part(target, i, j), pass_send.at[i, j], pass_recv.at[i, j], range=to)

    def edge_hop(f, source, target, to):
        return remote(source.at[f], target.at[f], edge_pass_send.at[f], edge_pass_recv.at[f], range=to)

    edge_copy = remote(edge_out, edge_in, edge_send, edge_recv, range=r - 1)

    pl.semaphore_wait(
        barrier,
        one(plain_out) + one(seam_out) + 3 * one(seam_in) + one(second_stop)
        + one(jnp.logical_and(first_stop, z >= 2))
        + one(d > 0) + one(d < n_depth - 1),
    )

    up = remote(
        ext.at[:, pl.ds(HALO, HALO)], ext.at[:, pl.ds(HALO + height, HALO)],
        halo_send.at[0], halo_recv.at[0], depth=d - 1,
    )
    down = remote(
        ext.at[:, pl.ds(height, HALO)], ext.at[:, pl.ds(0, HALO)],
        halo_send.at[1], halo_recv.at[1], depth=d + 1,
    )

    @pl.when(d > 0)
    def _():
        up.start()

    @pl.when(d < n_depth - 1)
    def _():
        down.start()

    greet(seam_in, ready_wrap, range=r - RING + 1)
    for t in (1, 2, 3):
        greet(jnp.logical_and(first_stop, z == t), ready_next.at[t - 1], range=r - t)
        greet(seam_in, ready_next.at[0], range=r - t)
    greet(second_stop, ready_next.at[0], range=r + RING - 3)

    zeros = jnp.zeros((HALO, 128), jnp.float32)

    @pl.when(d == 0)
    def _():
        for f in range(4):
            ext[f, pl.ds(0, HALO)] = zeros
        ext[4, pl.ds(0, HALO)] = zeros + 1.0

    @pl.when(d == n_depth - 1)
    def _():
        for f in range(4):
            ext[f, pl.ds(HALO + height, HALO)] = zeros
        last = ext[4, pl.ds(height, HALO)]
        ext[4, pl.ds(HALO + height, HALO)] = jnp.broadcast_to(last[HALO - 1 :], (HALO, 128))

    def interior(i, carry):
        main_chunk(i)

        @pl.when(plain_out)
        def _():
            tail_copy(i).start()

        @pl.when(jnp.logical_and(seam_out, i > FAR))
        def _():
            low_copy(i).start()

        @pl.when(jnp.logical_and(seam_out, i <= 2))
        def _():
            @pl.when(i == 1)
            def _():
                pl.semaphore_wait(ready_next.at[0], 1)

            for j in range(2):
                hop(i, j, tail_out, relay, r + 1).start()

        @pl.when(jnp.logical_and(seam_out, jnp.logical_and(i >= 3, i <= FAR)))
        def _():
            @pl.when(i == 3)
            def _():
                pl.semaphore_wait(ready_next.at[1], 1)

            for j in range(2):
                hop(i, j, tail_out, relay, r + 2).start()

        return carry

    lax.fori_loop(1, 4, interior, 0)

    @pl.when(d < n_depth - 1)
    def _():
        up.wait_recv()

    @pl.when(d > 0)
    def _():
        down.wait_recv()

    fold = span // 2
    high = (lane % 16) >= 8

    def fold_edge(load, target, first):
        def body(f, carry):
            packed = pack_columns(lambda g: load(f, g), lane, 0, 8)
            target[f + first] = jnp.where(high[:fold], packed[:fold], pltpu.roll(packed[fold:], 120, 1))
            return carry

        return body

    @pl.when(r > 0)
    def _():
        lax.fori_loop(0, 5, fold_edge(lambda f, g: ext[f, pl.ds(g * ROWS, span)], edge_out, 0), 0)

    @pl.when(plain_out)
    def _():
        edge_copy.start()

    @pl.when(seam_out)
    def _():
        pl.semaphore_wait(ready_next.at[2], 1)
        for f in range(5):
            edge_hop(f, edge_out, relay_edge, r + 3).start()

    lax.fori_loop(4, chunks - 1, interior, 0)

    def rim(i, carry):
        main_chunk(i * (chunks - 1))

        @pl.when(plain_out)
        def _():
            tail_copy(i * (chunks - 1)).start()

        @pl.when(seam_out)
        def _():
            low_copy(i * (chunks - 1)).start()

        return carry

    lax.fori_loop(0, 2, rim, 0)

    @pl.when(at_end)
    def _():
        for copy in far_loads:
            copy.wait()

        def turn_block(i, carry):
            at = pl.multiple_of(i * ROWS, ROWS)
            for f, fill in enumerate((0.0, 1.0)):
                block = raw[f, :, pl.ds(at, ROWS)]
                block = jnp.concatenate([block, jnp.full((128 - TAIL, ROWS), fill, jnp.float32)], 0)
                beyond[f, pl.ds(HALO + at, ROWS)] = block.T
            return carry

        lax.fori_loop(0, chunks, turn_block, 0)
        far_up = remote(
            beyond.at[:, pl.ds(HALO, HALO)], beyond.at[:, pl.ds(HALO + height, HALO)],
            far_send.at[0], far_recv.at[0], depth=d - 1,
        )
        far_down = remote(
            beyond.at[:, pl.ds(height, HALO)], beyond.at[:, pl.ds(0, HALO)],
            far_send.at[1], far_recv.at[1], depth=d + 1,
        )

        @pl.when(d > 0)
        def _():
            far_up.start()

        @pl.when(d < n_depth - 1)
        def _():
            far_down.start()

        @pl.when(d == 0)
        def _():
            beyond[0, pl.ds(0, HALO)] = zeros
            beyond[1, pl.ds(0, HALO)] = zeros + 1.0

        @pl.when(d == n_depth - 1)
        def _():
            beyond[0, pl.ds(HALO + height, HALO)] = zeros
            last = beyond[1, pl.ds(height, HALO)]
            beyond[1, pl.ds(HALO + height, HALO)] = jnp.broadcast_to(last[HALO - 1 :], (HALO, 128))

        @pl.when(d < n_depth - 1)
        def _():
            far_up.wait_recv()

        @pl.when(d > 0)
        def _():
            far_down.wait_recv()

        nothing = jnp.zeros((span, 128), jnp.float32)

        def far_out(i):
            return pltpu.make_async_copy(relay.at[i], tail.at[i], pass_send.at[i, 0])

        def far_chunk(i, carry):
            at = pl.multiple_of(i * ROWS, ROWS)
            fields = [nothing] * 3 + [beyond[f, pl.ds(at, span)] for f in range(2)]
            row = iota_row + (row_start - HALO + at)
            results = advance(fields, row, lane + full, offsets, [], full, False, True)
            pack_tail(i, results, relay)
            far_out(i).start()
            return carry

        lax.fori_loop(0, chunks, far_chunk, 0)
        for i in range(chunks):
            far_out(i).wait()
        for f in range(3):
            edge_in[f] = nothing[:fold]
        lax.fori_loop(0, 2, fold_edge(lambda f, g: beyond[f, pl.ds(g * ROWS, span)], edge_in, 3), 0)

        @pl.when(d > 0)
        def _():
            far_up.wait_send()

        @pl.when(d < n_depth - 1)
        def _():
            far_down.wait_send()

    near = [i for i in range(chunks) if not 1 <= i <= FAR]

    @pl.when(base)
    def _():
        pl.semaphore_wait(ready_wrap, 1)
        for i in near[1:-1] + [near[0], near[-1]]:
            low_copy(i).wait_recv()
            wrap_copy(i).start()

    leg = jnp.where(z >= 4, z - 3, z)
    first_chunk = jnp.where(leg == 1, 1, 3)
    last_chunk = jnp.where(leg == 1, 3, jnp.where(leg == 2, FAR + 1, 3))
    to = jnp.where(first_stop, r - RING + 3, r + RING - 1 - z)
    passes = jnp.logical_or(first_stop, second_stop)

    @pl.when(passes)
    def _():
        pl.semaphore_wait(ready_next.at[0], 1)

        def pass_on(i, carry):
            for j in range(2):
                hop(i, j, relay, relay, to).wait_recv()

                @pl.when(first_stop)
                def _():
                    hop(i, j, relay, relay, to).start()

                @pl.when(second_stop)
                def _():
                    hop(i, j, relay, tail, to).start()

            return carry

        lax.fori_loop(first_chunk, last_chunk, pass_on, 0)

        @pl.when(leg == 3)
        def _():
            for f in range(5):
                edge_hop(f, relay_edge, relay_edge, to).wait_recv()

                @pl.when(first_stop)
                def _():
                    edge_hop(f, relay_edge, relay_edge, to).start()

                @pl.when(second_stop)
                def _():
                    edge_hop(f, relay_edge, edge_in, to).start()

    @pl.when(plain_in)
    def _():
        edge_copy.wait_recv()

    @pl.when(seam_in)
    def _():
        for f in range(5):
            edge_hop(f, relay_edge, edge_in, r).wait_recv()

    def own_edge(f, carry):
        packed = pack_columns(lambda g: ext[f, pl.ds(g * ROWS, span)], lane, 120, 0)
        folded = edge_in[f]
        other = jnp.concatenate([folded, pltpu.roll(folded, 8, 1)], 0)
        seam[f] = jnp.where(high, other, packed)
        return carry

    lax.fori_loop(0, 5, own_edge, 0)
    row = iota_row + (row_start - HALO) + ROWS * (lane // 16)
    results = advance(
        [seam[f] for f in range(5)], row, 128 * r + 120 + lane % 16, offsets, points, full, False, True
    )
    for f, value in enumerate(results):
        strip_out[f] = value[HALO : HALO + ROWS]
    strip_copy = pltpu.make_async_copy(strip_out, strip, strip_sem)
    strip_copy.start()

    @pl.when(plain_in)
    def _():
        for i in range(chunks):
            tail_copy(i).wait_recv()

    @pl.when(seam_in)
    def _():
        for i in near:
            tail_copy(i).wait_recv()
        for i in range(1, FAR + 1):
            for j in range(2):
                hop(i, j, relay, tail, r).wait_recv()

    @pl.when(plain_out)
    def _():
        edge_copy.wait_send()
        for i in range(chunks):
            tail_copy(i).wait_send()

    @pl.when(seam_out)
    def _():
        for i in near:
            low_copy(i).wait_send()
        for i in range(1, FAR + 1):
            for j in range(2):
                hop(i, j, tail_out, relay, r).wait_send()
        for f in range(5):
            edge_hop(f, edge_out, relay_edge, r).wait_send()

    @pl.when(base)
    def _():
        for i in near:
            wrap_copy(i).wait_send()

    @pl.when(passes)
    def _():
        def passed(i, carry):
            for j in range(2):
                hop(i, j, relay, relay, r).wait_send()
            return carry

        lax.fori_loop(first_chunk, last_chunk, passed, 0)

        @pl.when(leg == 3)
        def _():
            for f in range(5):
                edge_hop(f, relay_edge, relay_edge, r).wait_send()

    strip_copy.wait()
    for i in range(chunks):
        main_copy(i).wait()

    @pl.when(d > 0)
    def _():
        up.wait_send()

    @pl.when(d < n_depth - 1)
    def _():
        down.wait_send()


def finish(main_in, tail_in, strip_in, shifts, p_out, vr_out, vz_out, main, tail, strip, out, in_sem, strip_sem, sem):
    chunks = tail.shape[0]

    def rows(i):
        return pl.ds(pl.multiple_of(i * ROWS, ROWS), ROWS)

    strip_copy = pltpu.make_async_copy(strip_in, strip, strip_sem)
    strip_copy.start()

    def loads(i):
        return (
            pltpu.make_async_copy(main_in.at[:, rows(i)], main.at[:, rows(i)], in_sem.at[i, 0]),
            pltpu.make_async_copy(tail_in.at[i], tail.at[i], in_sem.at[i, 1]),
        )

    for i in range(chunks):
        for copy in loads(i):
            copy.start()
    offset = shifts[0]
    for t in range(1, ITERS):
        offset = offset + shifts[t]
    half = ROWS // 2
    lane = lax.broadcasted_iota(jnp.int32, (half, 128), 1)
    outs = (p_out, vr_out, vz_out)

    def store(i, f):
        return pltpu.make_async_copy(out.at[f, rows(i)], outs[f].at[rows(i)], sem.at[i, f])

    strip_copy.wait()

    def body(i, carry):
        for copy in loads(i):
            copy.wait()
        for f in range(3):
            packed = tail[i, f]
            for h in range(2):
                at = pl.ds(pl.multiple_of(i * ROWS + h * half, half), half)
                edge = pltpu.roll(strip[f, h * half : (h + 1) * half], 248 - 16 * i, 1)
                near = jnp.where(lane >= 124, edge, main[f, at])
                far = packed if h == 0 else pltpu.roll(packed, TAIL, 1)
                far = jnp.where(lane < 4, edge, far)
                out[f, at] = pltpu.roll(jnp.where(lane >= offset, near, far), 128 - offset, 1)
            store(i, f).start()
        return carry

    lax.fori_loop(0, chunks, body, 0)
    for i in range(chunks):
        for f in range(3):
            store(i, f).wait()


def solution(mesh):
    n_range, n_depth = mesh.shape["range"], mesh.shape["depth"]

    def step(p, vr, vz, c, rho, ac, ad, shifts, sources, wavelet):
        height = p.shape[0]
        chunks = height // ROWS
        span = ROWS + 2 * HALO
        f32 = jnp.float32
        dma = pltpu.SemaphoreType.DMA
        hbm = pl.BlockSpec(memory_space=pltpu.HBM)
        smem = pl.BlockSpec(memory_space=pltpu.SMEM)
        main, tail, strip = pl.pallas_call(
            functools.partial(kernel, n_range, n_depth),
            out_shape=(
                jax.ShapeDtypeStruct((3, height, 128), f32),
                jax.ShapeDtypeStruct((chunks, 3, ROWS // 2, 128), f32),
                jax.ShapeDtypeStruct((3, ROWS, 128), f32),
            ),
            in_specs=[hbm] * 7 + [smem] * 3,
            out_specs=(hbm, hbm, hbm),
            scratch_shapes=[
                pltpu.VMEM((5, height + 2 * HALO, 128), f32),
                pltpu.VMEM((2, height + 2 * HALO, 128), f32),
                pltpu.VMEM((2, 64, height), f32),
                pltpu.VMEM((chunks, 3, ROWS // 2, 128), f32),
                pltpu.VMEM((5, span // 2, 128), f32),
                pltpu.VMEM((5, span // 2, 128), f32),
                pltpu.VMEM((chunks, 3, ROWS // 2, 128), f32),
                pltpu.VMEM((5, span // 2, 128), f32),
                pltpu.VMEM((5, span, 128), f32),
                pltpu.VMEM((3, height, 128), f32),
                pltpu.VMEM((3, ROWS, 128), f32),
                dma((5,)), dma((2,)), dma((2,)), dma((2,)), dma((2,)), dma((2,)),
                dma, dma, dma((chunks,)), dma((chunks,)), dma((chunks, 2)), dma((chunks, 2)), dma((5,)), dma((5,)),
                pltpu.SemaphoreType.REGULAR, pltpu.SemaphoreType.REGULAR((3,)), dma((chunks,)), dma,
            ],
            compiler_params=pltpu.CompilerParams(
                collective_id=1, has_side_effects=True, vmem_limit_bytes=58 * 2**20
            ),
        )(p, vr, vz, c, rho, ac.T, ad.T, shifts, sources.T, wavelet.T)
        block = jax.ShapeDtypeStruct((height, 128), f32)
        return pl.pallas_call(
            finish,
            out_shape=(block, block, block),
            in_specs=[hbm, hbm, hbm, smem],
            out_specs=(hbm, hbm, hbm),
            scratch_shapes=[
                pltpu.VMEM((3, height, 128), f32),
                pltpu.VMEM((chunks, 3, ROWS // 2, 128), f32),
                pltpu.VMEM((3, ROWS, 128), f32),
                pltpu.VMEM((3, height, 128), f32),
                dma((chunks, 2)), dma, dma((chunks, 3)),
            ],
            compiler_params=pltpu.CompilerParams(vmem_limit_bytes=58 * 2**20),
        )(main, tail, strip, shifts)

    block = P("depth", "range")
    return jax.shard_map(
        step,
        mesh=mesh,
        in_specs=(block,) * 5 + (P("depth", None),) * 2 + (P(),) * 3,
        out_specs=(block, block, block),
        check_vma=False,
    )
```

time: 66.7 us -> 44.9 us (0.67)
  the two profiles are of different devices: /device:TPU:54 before, /device:TPU:464 now
where the time goes in v2:
time: 44.9 us; the launch traced here: 44.6 us
  Pallas kernels  44 us (98%)
  between operations  0.64 us (1%)
    pallas_call x1, Pallas kernels, step(): pl.pallas_call(functools.partial(kernel, n_range, n_depth), out_shape=(ja...  38.5 us
    pallas_call x1, Pallas kernels, step(): pl.pallas_call(finish, out_shape=(block, block, block), in_specs=[hbm, hb...  5.5 us

profile of v2, /device:TPU:464, one launch (start us, length us, event | category | flops | bytes accessed | tf_op | source)
XLA Modules:
  0.0 44.6 jit_solution(13762502918387981889)
XLA Ops:
  0.6 38.5 %shard_map.121 = (f32[3,1024,128]{2,1,0:T(8,128)}, f32[8,3,64,128]{3,2,1,0:T(8,128)}, f32[3,128,128]{2,1,0:T(8,128)}) custom-call(f32[1024,128]{1,0:T(8,128)} %p_in.1, f32[1024,128]{1,0:T(8,128)} %vr_in.1, f32[1024,128]{1,0:T(8,128)} %vz_in.1, f32[1024,128]{1,0:T(8,128)} %c_in.1, f32[1024,128]{1,0:T(8,128)} %rho_in.1, f32[64,1024]{1,0:T(8,128)} %bitcast.4, ...), custom_call_target="tpu_custom_call" | custom-call | tf_op jit(solution)/shard_map/pallas_call | solution.py:594
  39.1 5.5 %shard_map.122 = (f32[1024,128]{1,0:T(8,128)}, f32[1024,128]{1,0:T(8,128)}, f32[1024,128]{1,0:T(8,128)}) custom-call(f32[3,1024,128]{2,1,0:T(8,128)} %get-tuple-element.6.main_in, f32[8,3,64,128]{3,2,1,0:T(8,128)} %get-tuple-element.7.tail_in, f32[3,128,128]{2,1,0:T(8,128)} %get-tuple-element.8.strip_in, s32[4]{0:T(128)} %shifts.3), custom_call_target="tpu_custom_call" | custom-call | tf_op jit(solution)/shard_map/pallas_call | solution.py:624
